TPU v7x, 32 devices: a whole 2x2x4 slice. The times are simulated.
32 devices in a mesh: ctx: 8 (over y, x, core), head: 4 (over z).
Axes of the slice: x: 2, y: 2, z: 4, core: 2. Of those that a mesh axis runs over, the one named last changes fastest.
Arguments:
- tokens: bfloat16 [1024, 4096], P('ctx'), may hold values from -8 to 8
- w_query: bfloat16 [4096, 4096], P(None, 'head'), may hold values from -1 to 1
- w_key: bfloat16 [4096, 1024], P(None, 'head'), may hold values from -1 to 1
- w_value: bfloat16 [4096, 1024], P(None, 'head'), may hold values from -0.09375 to 0.09375
- w_out: bfloat16 [4096, 4096], P('head'), may hold values from -0.09375 to 0.09375
- doc_ids: int32 [1024], P('ctx'), may hold values from 0 to 7, never falling along the last dimension, each value on 1 to 640 neighbouring positions
Outputs:
- mixed: bfloat16 [1024, 4096], P('ctx', 'head')
Inputs may be any that keep to these rules, and one draw needn't show every extreme that they name: doc_ids never fall along the context; each document has 1 to 640 tokens and one has exactly 640.
All inputs are finite; a program needn't handle non-finite values.
Results may differ from a plain program's by a relative error of at most 0.011.
Values may be sent and summed in bfloat16 or wider, within the bound.
A program may use at most 128 MiB of HBM per device.

v0:
```python
import functools
import math

import jax
import jax.numpy as jnp
import numpy as np
from jax import lax
from jax.experimental import pallas as pl
from jax.experimental.pallas import tpu as pltpu
from jax.sharding import PartitionSpec as P

HD = 128
STEPS = 4
SUB = 2
MESH = pl.DeviceIdType.MESH


def kernel(
    n_ctx, n_head,
    tokens, w_query, w_key, w_value, w_out, docs, freqs, out,
    tok, wq, wk, wv, wo, freq, doc_all, kv, q_acc, kv_acc, q, cos_ref, sin_ref, doc_q,
    sc, top, tot, acc, att, part, rbuf,
    tok_sem, wq_sem, wk_sem, wv_sem, wo_sem, small_sem,
    kv_send, kv_fwd, kv_recv, part_send, part_recv,
):
    rows = tokens.shape[0]
    kv_heads = w_key.shape[1] // HD
    heads = w_query.shape[1] // HD
    group = heads // kv_heads
    kv_width = kv_heads * HD
    chips = n_ctx // 2
    me = lax.axis_index("ctx")
    z = lax.axis_index("head")
    core = lax.rem(me, 2)
    chip = me // 2
    partner = me + 1 - 2 * core
    step_rows = wq.shape[1]
    piece = wo.shape[2]

    def tok_copy(c):
        return pltpu.make_async_copy(
            tokens.at[:, pl.ds(pl.multiple_of(c * step_rows, step_rows), step_rows)],
            tok.at[c], tok_sem.at[c])

    def rows_copy(src, dst, sem, c):
        return pltpu.make_async_copy(
            src.at[pl.ds(pl.multiple_of(c * step_rows, step_rows), step_rows), :],
            dst.at[c], sem.at[c])

    def wo_copy(p):
        return pltpu.make_async_copy(
            w_out.at[:, pl.ds(pl.multiple_of(p * piece, piece), piece)], wo.at[p], wo_sem.at[p])

    doc_copy = pltpu.make_async_copy(docs, doc_all.at[me], small_sem.at[0])
    freq_copy = pltpu.make_async_copy(freqs, freq, small_sem.at[1])

    def piece_of(k):
        return jnp.where(z < n_head // 2, n_head * SUB - 1 - k, k)

    doc_copy.start()
    freq_copy.start()
    for c in range(STEPS):
        tok_copy(c).start()
        rows_copy(w_key, wk, wk_sem, c).start()
        rows_copy(w_value, wv, wv_sem, c).start()
    rows_copy(w_query, wq, wq_sem, 0).start()

    barrier = pltpu.get_barrier_semaphore()

    def greet(c, carry):
        @pl.when(c != chip)
        def _():
            pl.semaphore_signal(
                barrier, inc=1, device_id={"ctx": c * 2 + core}, device_id_type=MESH)
        return carry

    lax.fori_loop(0, chips, greet, 0)
    pl.semaphore_signal(barrier, inc=1, device_id={"ctx": partner}, device_id_type=MESH)

    @pl.when(z > 0)
    def _():
        pl.semaphore_signal(barrier, inc=1, device_id={"head": z - 1}, device_id_type=MESH)

    @pl.when(z < n_head - 1)
    def _():
        pl.semaphore_signal(barrier, inc=1, device_id={"head": z + 1}, device_id_type=MESH)

    freq_copy.wait()
    doc_copy.wait()
    places = (me * rows + lax.broadcasted_iota(jnp.int32, (rows, HD), 0)).astype(jnp.float32)
    angles = places * freq[...]
    lane = lax.broadcasted_iota(jnp.int32, (rows, HD), 1)
    cos_ref[...] = jnp.cos(angles)
    sine = jnp.sin(angles)
    sin_ref[...] = jnp.where(lane < HD // 2, -sine, sine)
    doc_q[...] = jnp.broadcast_to(doc_all[me].astype(jnp.float32), (rows, rows)).T

    def rotated(x):
        return (x * cos_ref[...] + pltpu.roll(x, HD // 2, 1) * sin_ref[...]).astype(jnp.bfloat16)

    kv_acc[...] = jnp.zeros_like(kv_acc)

    def kv_step(c, carry):
        tok_copy(c).wait()
        rows_copy(w_key, wk, wk_sem, c).wait()
        rows_copy(w_value, wv, wv_sem, c).wait()

        @pl.when(c > 0)
        def _():
            rows_copy(w_query, wq, wq_sem, c).start()
        kv_acc[:, :kv_width] += jnp.dot(tok[c], wk[c], preferred_element_type=jnp.float32)
        kv_acc[:, kv_width:] += jnp.dot(tok[c], wv[c], preferred_element_type=jnp.float32)
        return carry

    lax.fori_loop(0, STEPS, kv_step, 0)
    for h in range(kv_heads):
        kv[me, :, h * HD:(h + 1) * HD] = rotated(kv_acc[:, h * HD:(h + 1) * HD])
    kv[me, :, kv_width:] = kv_acc[:, kv_width:].astype(jnp.bfloat16)

    pl.semaphore_wait(
        barrier,
        chips + (z > 0).astype(jnp.int32) + (z < n_head - 1).astype(jnp.int32))

    def block_copies(block, sems, slot, target):
        return [
            pltpu.make_async_remote_copy(
                src_ref=ref.at[block], dst_ref=ref.at[block],
                send_sem=sems.at[i, slot], recv_sem=kv_recv.at[i, block],
                device_id={"ctx": target}, device_id_type=MESH)
            for i, ref in enumerate((kv, doc_all))
        ]

    def send_one(i, carry):
        c = chips - 1 - i
        for copy in block_copies(me, kv_send, c, c * 2 + core):
            copy.start()
        return carry

    lax.fori_loop(0, chips - 1 - chip, send_one, 0)

    @pl.when(core == 0)
    def _():
        for copy in block_copies(me, kv_send, chip, partner):
            copy.start()

    q_acc[...] = jnp.zeros_like(q_acc)

    def q_step(c, carry):
        rows_copy(w_query, wq, wq_sem, c).wait()
        for i in range(n_head * SUB // STEPS):
            wo_copy(piece_of(c * (n_head * SUB // STEPS) + i)).start()
        q_acc[...] += jnp.dot(tok[c], wq[c], preferred_element_type=jnp.float32)
        return carry

    lax.fori_loop(0, STEPS, q_step, 0)
    for h in range(heads):
        q[h] = rotated(q_acc[:, h * HD:(h + 1) * HD])

    def score_block(j, own):
        ok = doc_q[...] == doc_all[j].astype(jnp.float32)
        if own:
            ok = ok & (lane <= lax.broadcasted_iota(jnp.int32, (rows, rows), 0))
        bias = jnp.where(ok, 0.0, -1e30).astype(jnp.float32)
        for h in range(kv_heads):
            s = lax.dot_general(
                q[h * group:(h + 1) * group].reshape(group * rows, HD),
                kv[j, :, h * HD:(h + 1) * HD],
                (((1,), (1,)), ((), ())), preferred_element_type=jnp.float32)
            s = (s.reshape(group, rows, rows) + bias[None]).reshape(group * rows, rows)
            sc[j, h] = s
            top[h] = s if own else jnp.maximum(top[h], s)

    score_block(me, True)

    def wait_block(j):
        for copy in block_copies(j, kv_fwd, 0, partner):
            copy.wait_recv()

    @pl.when(core == 1)
    def _():
        wait_block(me - 1)
        score_block(me - 1, False)

    def chip_step(i, carry):
        s = chip - 1 - i
        mine = s * 2 + core
        wait_block(mine)
        for copy in block_copies(mine, kv_fwd, s, partner):
            copy.start()
        score_block(mine, False)
        other = s * 2 + 1 - core
        wait_block(other)
        score_block(other, False)
        return carry

    lax.fori_loop(0, chip, chip_step, 0)

    factor = math.log2(math.e) / math.sqrt(HD)
    for h in range(kv_heads):
        top[h] = jnp.broadcast_to(jnp.max(top[h], axis=1, keepdims=True), top.shape[1:])
    tot[...] = jnp.zeros_like(tot)
    acc[...] = jnp.zeros_like(acc)

    def weigh(j, carry):
        for h in range(kv_heads):
            p = jnp.exp2((sc[j, h] - top[h]) * factor)
            tot[h] += p
            acc[h] += jnp.dot(
                p.astype(jnp.bfloat16), kv[j, :, kv_width + h * HD:kv_width + (h + 1) * HD],
                preferred_element_type=jnp.float32)
        return carry

    lax.fori_loop(0, me + 1, weigh, 0)
    for h in range(kv_heads):
        result = (acc[h] / jnp.sum(tot[h], axis=1, keepdims=True)).astype(jnp.bfloat16)
        for g in range(group):
            att[:, (h * group + g) * HD:(h * group + g + 1) * HD] = result[g * rows:(g + 1) * rows]

    def piece_copy(p, way):
        target = z + 1 if way == 0 else z - 1
        return pltpu.make_async_remote_copy(
            src_ref=part.at[p], dst_ref=rbuf.at[way, p],
            send_sem=part_send.at[p], recv_sem=part_recv.at[way, p],
            device_id={"head": target}, device_id_type=MESH)

    def project(k, carry):
        p = piece_of(k)
        wo_copy(p).wait()
        part[p] = jnp.dot(att[...], wo[p], preferred_element_type=jnp.float32).astype(jnp.bfloat16)

        @pl.when((z == 0) & (p >= SUB))
        def _():
            piece_copy(p, 0).start()

        @pl.when((z == n_head - 1) & (p < (n_head - 1) * SUB))
        def _():
            piece_copy(p, 1).start()
        return carry

    lax.fori_loop(0, n_head * SUB, project, 0)

    def pass_on(p, way):
        piece_copy(p, way).wait_recv()
        part[p] = (part[p].astype(jnp.float32) + rbuf[way, p].astype(jnp.float32)).astype(jnp.bfloat16)
        piece_copy(p, way).start()

    def relay(t, carry):
        a = t - z
        b = t - (n_head - 1 - z)

        @pl.when((z > 0) & (a >= 0) & (a < SUB * (n_head - 1 - z)))
        def _():
            pass_on(n_head * SUB - 1 - a, 0)

        @pl.when((z < n_head - 1) & (b >= 0) & (b < SUB * z))
        def _():
            pass_on(b, 1)
        return carry

    @pl.when((z > 0) & (z < n_head - 1))
    def _():
        lax.fori_loop(0, SUB * (n_head - 1) + n_head, relay, 0)

    def last(s, add_left, add_right):
        p = z * SUB + s
        value = part[p].astype(jnp.float32)
        if add_left:
            piece_copy(p, 0).wait_recv()
            value += rbuf[0, p].astype(jnp.float32)
        if add_right:
            piece_copy(p, 1).wait_recv()
            value += rbuf[1, p].astype(jnp.float32)
        out[:, s * piece:(s + 1) * piece] = value.astype(jnp.bfloat16)

    for which, left, right in ((z == 0, False, True), (z == n_head - 1, True, False),
                               ((z > 0) & (z < n_head - 1), True, True)):
        @pl.when(which)
        def _(left=left, right=right):
            for s in reversed(range(SUB)) if left else range(SUB):
                last(s, left, right)

    def drain_one(c, carry):
        for copy in block_copies(me, kv_send, c, c * 2 + core):
            copy.wait_send()
        return carry

    lax.fori_loop(chip + 1, chips, drain_one, 0)

    @pl.when(core == 0)
    def _():
        for copy in block_copies(me, kv_send, chip, partner):
            copy.wait_send()

    def drain_forward(s, carry):
        for copy in block_copies(s * 2 + core, kv_fwd, s, partner):
            copy.wait_send()
        return carry

    lax.fori_loop(0, chip, drain_forward, 0)

    def drain_piece(p, carry):
        @pl.when((p < z * SUB) | (p >= (z + 1) * SUB))
        def _():
            piece_copy(p, 0).wait_send()
        return carry

    lax.fori_loop(0, n_head * SUB, drain_piece, 0)


def solution(mesh):
    n_ctx, n_head = mesh.shape["ctx"], mesh.shape["head"]
    half = HD // 2
    base = 500000.0 ** (-2.0 * np.arange(half, dtype=np.float64) / HD)
    table = np.concatenate([base, base]).astype(np.float32)[None, :]

    def step(tokens, w_query, w_key, w_value, w_out, doc_ids):
        rows, width = tokens.shape
        q_width, kv_width = w_query.shape[1], w_key.shape[1]
        kv_heads, heads = kv_width // HD, q_width // HD
        group = heads // kv_heads
        step_rows = width // STEPS
        out_width = w_out.shape[1]
        pieces = n_head * SUB
        piece = out_width // pieces
        bf16, f32 = jnp.bfloat16, jnp.float32
        dma = pltpu.SemaphoreType.DMA
        return pl.pallas_call(
            functools.partial(kernel, n_ctx, n_head),
            out_shape=jax.ShapeDtypeStruct((rows, out_width // n_head), bf16),
            in_specs=[pl.BlockSpec(memory_space=pl.ANY)] * 7,
            out_specs=pl.BlockSpec(memory_space=pltpu.VMEM),
            scratch_shapes=[
                pltpu.VMEM((STEPS, rows, step_rows), bf16),
                pltpu.VMEM((STEPS, step_rows, q_width), bf16),
                pltpu.VMEM((STEPS, step_rows, kv_width), bf16),
                pltpu.VMEM((STEPS, step_rows, kv_width), bf16),
                pltpu.VMEM((pieces, q_width, piece), bf16),
                pltpu.VMEM((1, HD), f32),
                pltpu.VMEM((n_ctx, 1, rows), jnp.int32),
                pltpu.VMEM((n_ctx, rows, 2 * kv_width), bf16),
                pltpu.VMEM((rows, q_width), f32),
                pltpu.VMEM((rows, 2 * kv_width), f32),
                pltpu.VMEM((heads, rows, HD), bf16),
                pltpu.VMEM((rows, HD), f32),
                pltpu.VMEM((rows, HD), f32),
                pltpu.VMEM((rows, rows), f32),
                pltpu.VMEM((n_ctx, kv_heads, group * rows, rows), f32),
                pltpu.VMEM((kv_heads, group * rows, rows), f32),
                pltpu.VMEM((kv_heads, group * rows, rows), f32),
                pltpu.VMEM((kv_heads, group * rows, HD), f32),
                pltpu.VMEM((rows, q_width), bf16),
                pltpu.VMEM((pieces, rows, piece), bf16),
                pltpu.VMEM((2, pieces, rows, piece), bf16),
                dma((STEPS,)), dma((STEPS,)), dma((STEPS,)), dma((STEPS,)), dma((pieces,)), dma((2,)),
                dma((2, n_ctx // 2)), dma((2, n_ctx // 2)), dma((2, n_ctx)),
                dma((pieces,)), dma((2, pieces)),
            ],
            compiler_params=pltpu.CompilerParams(
                collective_id=0, has_side_effects=True, vmem_limit_bytes=60 * 1024 * 1024),
            name="attention_layer",
        )(tokens, w_query, w_key, w_value, w_out, doc_ids.reshape(1, rows), jnp.asarray(table))

    return jax.shard_map(
        step,
        mesh=mesh,
        in_specs=(
            P("ctx", None),
            P(None, "head"),
            P(None, "head"),
            P(None, "head"),
            P("head", None),
            P("ctx"),
        ),
        out_specs=P("ctx", "head"),
        check_vma=False,
    )
```

profile of v0, /device:TPU:22, one launch (start us, length us, event | category | flops | bytes accessed | tf_op | source)
XLA Modules:
  0.0 38.4 jit_solution(10591884421511544220)
XLA Ops:
  0.0 36.7 %attention_layer.1 = bf16[128,1024]{1,0:T(8,128)(2,1)} custom-call(bf16[128,4096]{1,0:T(8,128)(2,1)} %tokens.1, bf16[4096,1024]{1,0:T(8,128)(2,1)} %w_query.1, bf16[4096,256]{1,0:T(8,128)(2,1)} %w_key.1, bf16[4096,256]{1,0:T(8,128)(2,1)} %w_value.1, bf16[1024,4096]{1,0:T(8,128)(2,1)} %w_out.1, s32[1,128]{1,0:T(1,128)} %bitcast.1, f32[1,128]{1,0:T(1,128)} %constant.2.clone.freqs), custom_call_target="tpu_custom_call" | custom-call | tf_op jit(solution)/shard_map/attention_layer/pallas_call | solution.py:327
  36.7 1.7 %copy.9 = bf16[128,1024]{1,0:T(8,128)(2,1)} copy(bf16[128,1024]{1,0:T(8,128)(2,1)} %attention_layer.1) | data formatting | bytes 524288
where the time goes:
time: 38.5 us; the launch traced here: 38.4 us
  Pallas kernels  36.7 us (95%)
  local copies, waits for them, and re-layouts  1.67 us (4%)
    pallas_call x1, Pallas kernels, step(): pl.pallas_call(functools.partial(kernel, n_ctx, n_head), out_shape=jax.Sh...  36.7 us
    unnamed x1, local copies, waits for them, and re-layouts  1.67 us

commit v1 on v0

v1 whole, which is shorter than its diff:
```python
import functools
import math

import jax
import jax.numpy as jnp
from jax import lax
from jax.experimental import pallas as pl
from jax.experimental.pallas import tpu as pltpu
from jax.sharding import PartitionSpec as P

HD = 128
BASE = 500000.0
STEPS = 4
SUB = 2
TAIL = 16
MESH = pl.DeviceIdType.MESH
FACTOR = math.log2(math.e) / math.sqrt(HD)


def kernel(
    n_ctx, n_head, reach,
    tokens, w_query, w_key, w_value, w_out, docs, out,
    tok, wq, wk, wv, wo, doc, kb, vb, q_acc, k_acc, v_acc, q, cos_ref, sin_ref, doc_q,
    top, tot, acc, att, part, rbuf,
    tok_sem, wk_sem, wv_sem, wq_sem, wo_sem, doc_sem,
    kv_send, kv_fwd, k_recv, v_recv, part_send, part_recv,
):
    rows = tokens.shape[0]
    kv_heads = w_key.shape[1] // HD
    heads = w_query.shape[1] // HD
    group = heads // kv_heads
    chips = n_ctx // 2
    near = (reach - 1) // 2
    me = lax.axis_index("ctx")
    z = lax.axis_index("head")
    core = lax.rem(me, 2)
    chip = me // 2
    partner = me + 1 - 2 * core
    step_rows = wq.shape[1]
    v_rows = wv.shape[1]
    piece = part.shape[2]

    def tok_copy(c):
        return pltpu.make_async_copy(
            tokens.at[:, c * step_rows:(c + 1) * step_rows], tok.at[c], tok_sem.at[c])

    def rows_copy(src, dst, sem, c):
        size = dst.shape[1]
        return pltpu.make_async_copy(src.at[c * size:(c + 1) * size, :], dst.at[c], sem.at[c])

    def wo_copy(t):
        width = SUB * piece
        return pltpu.make_async_copy(
            w_out.at[:, pl.ds(pl.multiple_of(t * width, width), width)], wo.at[t], wo_sem.at[t])

    def owner_of(k):
        return jnp.where(z < n_head // 2, n_head - 1 - k, k)

    doc_copy = pltpu.make_async_copy(docs, doc, doc_sem.at[0])
    doc_copy.start()
    for c in range(STEPS):
        tok_copy(c).start()
        rows_copy(w_key, wk, wk_sem, c).start()
    for c in range(STEPS // 2):
        rows_copy(w_value, wv, wv_sem, c).start()

    barrier = pltpu.get_barrier_semaphore()

    def greet(c, carry):
        @pl.when(c != chip)
        def _():
            pl.semaphore_signal(
                barrier, inc=1, device_id={"ctx": c * 2 + core}, device_id_type=MESH)
        return carry

    lax.fori_loop(0, chips, greet, 0)
    pl.semaphore_signal(barrier, inc=1, device_id={"ctx": partner}, device_id_type=MESH)
    gap = 2 * (near + 1) - 1

    @pl.when((core == 1) & (chip + near + 1 < chips))
    def _():
        pl.semaphore_signal(barrier, inc=1, device_id={"ctx": me + gap}, device_id_type=MESH)

    @pl.when((core == 0) & (chip > near))
    def _():
        pl.semaphore_signal(barrier, inc=1, device_id={"ctx": me - gap}, device_id_type=MESH)

    @pl.when(z > 0)
    def _():
        pl.semaphore_signal(barrier, inc=1, device_id={"head": z - 1}, device_id_type=MESH)

    @pl.when(z < n_head - 1)
    def _():
        pl.semaphore_signal(barrier, inc=1, device_id={"head": z + 1}, device_id_type=MESH)

    index = lax.broadcasted_iota(jnp.int32, (rows, HD), 1)
    freq = jnp.ones((rows, HD), jnp.float32)
    for b in range((HD // 2).bit_length() - 1):
        freq = freq * jnp.where(
            lax.rem(index // (1 << b), 2) == 1, jnp.float32(BASE ** (-2.0 * (1 << b) / HD)), 1.0)
    places = (me * rows + lax.broadcasted_iota(jnp.int32, (rows, HD), 0)).astype(jnp.float32)
    angles = places * freq
    cos_ref[...] = jnp.cos(angles)
    sine = jnp.sin(angles)
    sin_ref[...] = jnp.where(index < HD // 2, -sine, sine)

    def rotated(x):
        return (x * cos_ref[...] + pltpu.roll(x, HD // 2, 1) * sin_ref[...]).astype(jnp.bfloat16)

    for c in range(STEPS):
        tok_copy(c).wait()
        rows_copy(w_key, wk, wk_sem, c).wait()
        rows_copy(w_query, wq, wq_sem, c).start()
        product = jnp.dot(tok[c], wk[c], preferred_element_type=jnp.float32)
        k_acc[...] = product if c == 0 else k_acc[...] + product

    doc_copy.wait()
    doc_row = jnp.broadcast_to(doc[...].astype(jnp.float32), (rows, rows))
    doc_q[...] = doc_row.T
    kb[me, kv_heads * rows:, :] = doc_row[:TAIL].astype(jnp.bfloat16)
    for h in range(kv_heads):
        kb[me, h * rows:(h + 1) * rows, :] = rotated(k_acc[:, h * HD:(h + 1) * HD])

    pl.semaphore_wait(
        barrier,
        chips + (z > 0).astype(jnp.int32) + (z < n_head - 1).astype(jnp.int32)
        + ((core == 1) & (chip + near + 1 < chips)).astype(jnp.int32)
        + ((core == 0) & (chip > near)).astype(jnp.int32))

    def block_copy(ref, recv, send, block, target):
        return pltpu.make_async_remote_copy(
            src_ref=ref.at[block], dst_ref=ref.at[block],
            send_sem=send.at[0], recv_sem=recv.at[target - block - 1],
            device_id={"ctx": target}, device_id_type=MESH)

    def arrived(ref, recv, block):
        pltpu.make_async_remote_copy(
            src_ref=ref.at[block], dst_ref=ref.at[block],
            send_sem=kv_send.at[0], recv_sem=recv.at[me - block - 1],
            device_id={"ctx": partner}, device_id_type=MESH).wait_recv()

    last_near = jnp.minimum(chip + near, chips - 1)

    def own_targets(act):
        def one(c, carry):
            act(c * 2 + core)
            return carry

        lax.fori_loop(chip + 1, last_near + 1, one, 0)

        @pl.when(core == 0)
        def _():
            act(partner)

        @pl.when((core == 1) & (chip + near + 1 < chips))
        def _():
            act(me + gap)

    own_targets(lambda d: block_copy(kb, k_recv, kv_send, me, d).start())

    half = STEPS // 2
    for c in range(half):
        rows_copy(w_value, wv, wv_sem, c).wait()
        for i in range(STEPS // half):
            product = jnp.dot(
                tok[c * (STEPS // half) + i], wv[c, i * step_rows:(i + 1) * step_rows, :],
                preferred_element_type=jnp.float32)
            v_acc[...] = product if c == 0 and i == 0 else v_acc[...] + product
    vb[me] = v_acc[...].astype(jnp.bfloat16)
    own_targets(lambda d: block_copy(vb, v_recv, kv_send, me, d).start())

    for c in range(STEPS):
        rows_copy(w_query, wq, wq_sem, c).wait()
        if c < n_head:
            for k in range(c, n_head, STEPS):
                wo_copy(owner_of(k)).start()
        product = jnp.dot(tok[c], wq[c], preferred_element_type=jnp.float32)
        q_acc[...] = product if c == 0 else q_acc[...] + product
    for h in range(heads):
        q[h] = rotated(q_acc[:, h * HD:(h + 1) * HD])

    def block(j, own):
        ok = doc_q[...] == kb[j, kv_heads * rows:kv_heads * rows + 1, :].astype(jnp.float32)
        if own:
            ok = ok & (lax.broadcasted_iota(jnp.int32, (rows, rows), 1)
                       <= lax.broadcasted_iota(jnp.int32, (rows, rows), 0))
        bias = jnp.where(ok, 0.0, -1e30).astype(jnp.float32)
        for h in range(kv_heads):
            s = lax.dot_general(
                q[h * group:(h + 1) * group].reshape(group * rows, HD),
                kb[j, h * rows:(h + 1) * rows, :],
                (((1,), (1,)), ((), ())), preferred_element_type=jnp.float32)
            s = (s.reshape(group, rows, rows) + bias[None]).reshape(group * rows, rows)
            high = jnp.broadcast_to(jnp.max(s, axis=1, keepdims=True), s.shape)
            if not own:
                high = jnp.maximum(top[h], high)
                scale = jnp.exp2((top[h] - high) * FACTOR)
            p = jnp.exp2((s - high) * FACTOR)
            mixed = jnp.dot(
                p.astype(jnp.bfloat16), vb[j, :, h * HD:(h + 1) * HD],
                preferred_element_type=jnp.float32)
            top[h] = high
            tot[h] = p if own else tot[h] * scale + p
            acc[h] = mixed if own else acc[h] * scale + mixed

    block(me, True)

    @pl.when(core == 1)
    def _():
        arrived(kb, k_recv, me - 1)
        arrived(vb, v_recv, me - 1)
        block(me - 1, False)

    count = jnp.minimum(chip, near)

    def mine_of(i):
        return (chip - count + i) * 2 + core

    def other_of(i):
        return (chip - count + i) * 2 + 1 - core

    def pass_keys(i, carry):
        j = mine_of(i)
        arrived(kb, k_recv, j)

        block_copy(kb, k_recv, kv_fwd, j, partner).start()
        return carry

    lax.fori_loop(0, count, pass_keys, 0)

    def mine_step(i, carry):
        j = mine_of(i)
        arrived(vb, v_recv, j)
        block_copy(vb, v_recv, kv_fwd, j, partner).start()
        block(j, False)
        return carry

    lax.fori_loop(0, count, mine_step, 0)

    def other_step(i, carry):
        j = other_of(i)
        arrived(kb, k_recv, j)
        arrived(vb, v_recv, j)
        block(j, False)
        return carry

    lax.fori_loop(0, count, other_step, 0)

    @pl.when((core == 0) & (chip > near))
    def _():
        arrived(kb, k_recv, me - gap)
        arrived(vb, v_recv, me - gap)
        block(me - gap, False)

    for h in range(kv_heads):
        result = (acc[h] / jnp.sum(tot[h], axis=1, keepdims=True)).astype(jnp.bfloat16)
        for g in range(group):
            att[:, (h * group + g) * HD:(h * group + g + 1) * HD] = result[g * rows:(g + 1) * rows]

    def piece_copy(p, way):
        target = z + 1 if way == 0 else z - 1
        slot = p - SUB * target if way == 0 else SUB * (n_head - target) + p
        return pltpu.make_async_remote_copy(
            src_ref=part.at[p], dst_ref=rbuf.at[way, p],
            send_sem=part_send.at[0], recv_sem=part_recv.at[slot],
            device_id={"head": target}, device_id_type=MESH)

    def piece_arrived(p, way):
        slot = p - SUB * z if way == 0 else SUB * (n_head - z) + p
        pltpu.make_async_remote_copy(
            src_ref=part.at[p], dst_ref=rbuf.at[way, p],
            send_sem=part_send.at[0], recv_sem=part_recv.at[slot],
            device_id={"ctx": partner}, device_id_type=MESH).wait_recv()

    def project(k, carry):
        t = owner_of(k)
        wo_copy(t).wait()
        for s in range(SUB):
            p = t * SUB + s
            part[p] = jnp.dot(
                att[...], wo[t, :, s * piece:(s + 1) * piece],
                preferred_element_type=jnp.float32).astype(jnp.bfloat16)

            @pl.when((z == 0) & (t > 0))
            def _():
                piece_copy(p, 0).start()

            @pl.when((z == n_head - 1) & (t < n_head - 1))
            def _():
                piece_copy(p, 1).start()
        return carry

    lax.fori_loop(0, n_head, project, 0)

    def pass_on(p, way):
        piece_arrived(p, way)
        part[p] = (part[p].astype(jnp.float32) + rbuf[way, p].astype(jnp.float32)).astype(jnp.bfloat16)
        piece_copy(p, way).start()

    def relay(t, carry):
        a = t - z
        b = t - (n_head - 1 - z)

        @pl.when((z > 0) & (a >= 0) & (a < SUB * (n_head - 1 - z)))
        def _():
            pass_on((n_head - 1 - a // SUB) * SUB + lax.rem(a, SUB), 0)

        @pl.when((z < n_head - 1) & (b >= 0) & (b < SUB * z))
        def _():
            pass_on(b, 1)
        return carry

    @pl.when((z > 0) & (z < n_head - 1))
    def _():
        lax.fori_loop(0, SUB * (n_head - 1) + n_head, relay, 0)

    def last(s, add_left, add_right):
        p = z * SUB + s
        value = part[p].astype(jnp.float32)
        if add_left:
            piece_arrived(p, 0)
            value += rbuf[0, p].astype(jnp.float32)
        if add_right:
            piece_arrived(p, 1)
            value += rbuf[1, p].astype(jnp.float32)
        out[:, s * piece:(s + 1) * piece] = value.astype(jnp.bfloat16)

    own_targets(lambda d: block_copy(kb, k_recv, kv_send, me, d).wait_send())
    own_targets(lambda d: block_copy(vb, v_recv, kv_send, me, d).wait_send())

    def drain_forward(i, carry):
        block_copy(kb, k_recv, kv_fwd, mine_of(i), partner).wait_send()
        block_copy(vb, v_recv, kv_fwd, mine_of(i), partner).wait_send()
        return carry

    lax.fori_loop(0, count, drain_forward, 0)

    for which, left, right in ((z == 0, False, True), (z == n_head - 1, True, False),
                               ((z > 0) & (z < n_head - 1), True, True)):
        @pl.when(which)
        def _(left=left, right=right):
            for s in range(SUB):
                last(s, left, right)

    def drain_piece(p, carry):
        @pl.when((p < z * SUB) | (p >= (z + 1) * SUB))
        def _():
            pltpu.make_async_remote_copy(
                src_ref=part.at[p], dst_ref=rbuf.at[0, p],
                send_sem=part_send.at[0], recv_sem=part_recv.at[0],
                device_id={"ctx": partner}, device_id_type=MESH).wait_send()
        return carry

    lax.fori_loop(0, n_head * SUB, drain_piece, 0)


def solution(mesh):
    n_ctx, n_head = mesh.shape["ctx"], mesh.shape["head"]
    reach = n_ctx // 2 + 1

    def step(tokens, w_query, w_key, w_value, w_out, doc_ids):
        rows, width = tokens.shape
        q_width, kv_width = w_query.shape[1], w_key.shape[1]
        kv_heads, heads = kv_width // HD, q_width // HD
        group = heads // kv_heads
        step_rows = width // STEPS
        out_width = w_out.shape[1]
        pieces = n_head * SUB
        piece = out_width // pieces
        bf16, f32 = jnp.bfloat16, jnp.float32
        dma = pltpu.SemaphoreType.DMA
        return pl.pallas_call(
            functools.partial(kernel, n_ctx, n_head, reach),
            out_shape=pltpu.VMEM((rows, out_width // n_head), bf16),
            in_specs=[pl.BlockSpec(memory_space=pl.ANY)] * 6,
            out_specs=pl.BlockSpec(memory_space=pltpu.VMEM),
            scratch_shapes=[
                pltpu.VMEM((STEPS, rows, step_rows), bf16),
                pltpu.VMEM((STEPS, step_rows, q_width), bf16),
                pltpu.VMEM((STEPS, step_rows, kv_width), bf16),
                pltpu.VMEM((STEPS // 2, 2 * step_rows, kv_width), bf16),
                pltpu.VMEM((n_head, q_width, SUB * piece), bf16),
                pltpu.VMEM((1, rows), jnp.int32),
                pltpu.VMEM((n_ctx, kv_heads * rows + TAIL, HD), bf16),
                pltpu.VMEM((n_ctx, rows, kv_width), bf16),
                pltpu.VMEM((rows, q_width), f32),
                pltpu.VMEM((rows, kv_width), f32),
                pltpu.VMEM((rows, kv_width), f32),
                pltpu.VMEM((heads, rows, HD), bf16),
                pltpu.VMEM((rows, HD), f32),
                pltpu.VMEM((rows, HD), f32),
                pltpu.VMEM((rows, rows), f32),
                pltpu.VMEM((kv_heads, group * rows, rows), f32),
                pltpu.VMEM((kv_heads, group * rows, rows), f32),
                pltpu.VMEM((kv_heads, group * rows, HD), f32),
                pltpu.VMEM((rows, q_width), bf16),
                pltpu.VMEM((pieces, rows, piece), bf16),
                pltpu.VMEM((2, pieces, rows, piece), bf16),
                dma((STEPS,)), dma((STEPS,)), dma((STEPS // 2,)), dma((STEPS,)), dma((n_head,)), dma((1,)),
                dma((1,)), dma((1,)), dma((reach,)), dma((reach,)),
                dma((1,)), dma((SUB * (n_head + 1),)),
            ],
            compiler_params=pltpu.CompilerParams(
                collective_id=0, has_side_effects=True, vmem_limit_bytes=60 * 1024 * 1024),
            name="attention_layer",
        )(tokens, w_query, w_key, w_value, w_out, doc_ids.reshape(1, rows))

    return jax.shard_map(
        step,
        mesh=mesh,
        in_specs=(
            P("ctx", None),
            P(None, "head"),
            P(None, "head"),
            P(None, "head"),
            P("head", None),
            P("ctx"),
        ),
        out_specs=P("ctx", "head"),
        check_vma=False,
    )
```

time: 38.5 us -> 34.2 us (0.89)
  the two profiles are of different devices: /device:TPU:22 before, /device:TPU:12 now
where the time goes in v1:
time: 34.2 us; the launch traced here: 33.7 us
  Pallas kernels  33 us (96%)
  local copies, waits for them, and re-layouts  0.71 us (2%)
    pallas_call x1, Pallas kernels, step(): pl.pallas_call(functools.partial(kernel, n_ctx, n_head, reach), out_shape...  33 us
    unnamed x1, local copies, waits for them, and re-layouts  0.71 us

profile of v1, /device:TPU:12, one launch (start us, length us, event | category | flops | bytes accessed | tf_op | source)
XLA Modules:
  0.0 33.7 jit_solution(17733121981532584086)
XLA Ops:
  0.0 33.0 %attention_layer.1 = bf16[128,1024]{1,0:T(8,128)(2,1)S(1)} custom-call(bf16[128,4096]{1,0:T(8,128)(2,1)} %tokens.1, bf16[4096,1024]{1,0:T(8,128)(2,1)} %w_query.1, bf16[4096,256]{1,0:T(8,128)(2,1)} %w_key.1, bf16[4096,256]{1,0:T(8,128)(2,1)} %w_value.1, bf16[1024,4096]{1,0:T(8,128)(2,1)} %w_out.1, s32[1,128]{1,0:T(1,128)} %bitcast.1), custom_call_target="tpu_custom_call" | custom-call | tf_op jit(solution)/shard_map/attention_layer/pallas_call | solution.py:372
  33.0 0.7 %copy.8 = bf16[128,1024]{1,0:T(8,128)(2,1)} copy(bf16[128,1024]{1,0:T(8,128)(2,1)S(1)} %attention_layer.1) | data formatting | bytes 524288

commit v2 on v1

--- a/solution.py
+++ b/solution.py
@@ -11,7 +11,9 @@
 HD = 128
 BASE = 500000.0
 STEPS = 4
-SUB = 2
+SUB = 4
+SIDE = 2
+WIDE = 2
 TAIL = 16
 MESH = pl.DeviceIdType.MESH
 FACTOR = math.log2(math.e) / math.sqrt(HD)
@@ -20,10 +22,10 @@
 def kernel(
     n_ctx, n_head, reach,
     tokens, w_query, w_key, w_value, w_out, docs, out,
-    tok, wq, wk, wv, wo, doc, kb, vb, q_acc, k_acc, v_acc, q, cos_ref, sin_ref, doc_q,
-    top, tot, acc, att, part, rbuf,
+    tok, wq, wk, wv, wo, doc, kb, vb, q_acc, k_acc, v_acc, q, cos_ref, sin_ref,
+    top, tot, acc, att, part, rbuf, side,
     tok_sem, wk_sem, wv_sem, wq_sem, wo_sem, doc_sem,
-    kv_send, kv_fwd, k_recv, v_recv, part_send, part_recv,
+    kv_send, kv_fwd, k_recv, v_recv, part_send, part_recv, side_recv,
 ):
     rows = tokens.shape[0]
     kv_heads = w_key.shape[1] // HD
@@ -61,8 +63,6 @@
     for c in range(STEPS):
         tok_copy(c).start()
         rows_copy(w_key, wk, wk_sem, c).start()
-    for c in range(STEPS // 2):
-        rows_copy(w_value, wv, wv_sem, c).start()
 
     barrier = pltpu.get_barrier_semaphore()
 
@@ -76,6 +76,18 @@
     lax.fori_loop(0, chips, greet, 0)
     pl.semaphore_signal(barrier, inc=1, device_id={"ctx": partner}, device_id_type=MESH)
     gap = 2 * (near + 1) - 1
+    detour = chips == 4 and n_head == 4
+    helper, giver = chip == 0, chip == 2
+    greeted = chips + (z > 0).astype(jnp.int32) + (z < n_head - 1).astype(jnp.int32)
+    if detour:
+        for inner, edge in ((1, 0), (n_head - 2, n_head - 1)):
+            @pl.when(giver & (z == inner))
+            def _(edge=edge):
+                pl.semaphore_signal(
+                    barrier, inc=1, device_id={"ctx": me - n_ctx // 2, "head": edge},
+                    device_id_type=MESH)
+
+        greeted = greeted + (helper & ((z == 0) | (z == n_head - 1))).astype(jnp.int32)
 
     @pl.when((core == 1) & (chip + near + 1 < chips))
     def _():
@@ -110,21 +122,23 @@
     for c in range(STEPS):
         tok_copy(c).wait()
         rows_copy(w_key, wk, wk_sem, c).wait()
-        rows_copy(w_query, wq, wq_sem, c).start()
+        if c < STEPS // 2:
+            rows_copy(w_value, wv, wv_sem, c).start()
+        else:
+            for i in range(2 * c - STEPS, 2 * c - STEPS + 2):
+                rows_copy(w_query, wq, wq_sem, i).start()
         product = jnp.dot(tok[c], wk[c], preferred_element_type=jnp.float32)
         k_acc[...] = product if c == 0 else k_acc[...] + product
 
     doc_copy.wait()
-    doc_row = jnp.broadcast_to(doc[...].astype(jnp.float32), (rows, rows))
-    doc_q[...] = doc_row.T
-    kb[me, kv_heads * rows:, :] = doc_row[:TAIL].astype(jnp.bfloat16)
+    kb[me, kv_heads * rows:, :] = jnp.broadcast_to(
+        doc[...].astype(jnp.float32), (TAIL, rows)).astype(jnp.bfloat16)
     for h in range(kv_heads):
         kb[me, h * rows:(h + 1) * rows, :] = rotated(k_acc[:, h * HD:(h + 1) * HD])
 
     pl.semaphore_wait(
         barrier,
-        chips + (z > 0).astype(jnp.int32) + (z < n_head - 1).astype(jnp.int32)
-        + ((core == 1) & (chip + near + 1 < chips)).astype(jnp.int32)
+        greeted + ((core == 1) & (chip + near + 1 < chips)).astype(jnp.int32)
         + ((core == 0) & (chip > near)).astype(jnp.int32))
 
     def block_copy(ref, recv, send, block, target):
@@ -141,12 +155,22 @@
 
     last_near = jnp.minimum(chip + near, chips - 1)
 
+    relayed = ((chip == 1) & (core == 1)).astype(jnp.int32)
+    bearer = (chip == 3) & (core == 1)
+
     def own_targets(act):
         def one(c, carry):
             act(c * 2 + core)
             return carry
 
-        lax.fori_loop(chip + 1, last_near + 1, one, 0)
+        if detour:
+            lax.fori_loop(chip + 1, last_near + 1 - 2 * relayed, one, 0)
+
+            @pl.when(relayed == 1)
+            def _():
+                act(me + 4)
+        else:
+            lax.fori_loop(chip + 1, last_near + 1, one, 0)
 
         @pl.when(core == 0)
         def _():
@@ -166,7 +190,8 @@
                 tok[c * (STEPS // half) + i], wv[c, i * step_rows:(i + 1) * step_rows, :],
                 preferred_element_type=jnp.float32)
             v_acc[...] = product if c == 0 and i == 0 else v_acc[...] + product
-    vb[me] = v_acc[...].astype(jnp.bfloat16)
+    for h in range(kv_heads):
+        vb[me, h * HD:(h + 1) * HD, :] = v_acc[:, h * HD:(h + 1) * HD].T.astype(jnp.bfloat16)
     own_targets(lambda d: block_copy(vb, v_recv, kv_send, me, d).start())
 
     for c in range(STEPS):
@@ -177,39 +202,74 @@
         product = jnp.dot(tok[c], wq[c], preferred_element_type=jnp.float32)
         q_acc[...] = product if c == 0 else q_acc[...] + product
     for h in range(heads):
-        q[h] = rotated(q_acc[:, h * HD:(h + 1) * HD])
-
-    def block(j, own):
-        ok = doc_q[...] == kb[j, kv_heads * rows:kv_heads * rows + 1, :].astype(jnp.float32)
-        if own:
-            ok = ok & (lax.broadcasted_iota(jnp.int32, (rows, rows), 1)
-                       <= lax.broadcasted_iota(jnp.int32, (rows, rows), 0))
-        bias = jnp.where(ok, 0.0, -1e30).astype(jnp.float32)
+        g = h % group
+        q[h // group, g * rows:(g + 1) * rows, :] = rotated(q_acc[:, h * HD:(h + 1) * HD])
+
+    def attend(js, own, ready=None):
+        doc_row = doc[...].astype(jnp.float32)
+        biases = []
+        for i, j in enumerate(js):
+            column = kb[j, kv_heads * rows:kv_heads * rows + 1, :].astype(jnp.float32)
+            ok = jnp.broadcast_to(column, (rows, rows)).T == doc_row
+            if own and i == 0:
+                ok = ok & (lax.broadcasted_iota(jnp.int32, (rows, rows), 0)
+                           <= lax.broadcasted_iota(jnp.int32, (rows, rows), 1))
+            bias = jnp.where(ok, 0.0, -1e30).astype(jnp.float32)
+            biases.append(jnp.concatenate([bias] * group, axis=1))
+        scores = [
+            [bias + lax.dot_general(
+                kb[j, h * rows:(h + 1) * rows, :], q[h],
+                (((1,), (1,)), ((), ())), preferred_element_type=jnp.float32)
+             for j, bias in zip(js, biases)]
+            for h in range(kv_heads)]
+        scales, weights = [], []
         for h in range(kv_heads):
-            s = lax.dot_general(
-                q[h * group:(h + 1) * group].reshape(group * rows, HD),
-                kb[j, h * rows:(h + 1) * rows, :],
-                (((1,), (1,)), ((), ())), preferred_element_type=jnp.float32)
-            s = (s.reshape(group, rows, rows) + bias[None]).reshape(group * rows, rows)
-            high = jnp.broadcast_to(jnp.max(s, axis=1, keepdims=True), s.shape)
+            high = jnp.max(functools.reduce(jnp.maximum, scores[h]), axis=0, keepdims=True)
             if not own:
                 high = jnp.maximum(top[h], high)
-                scale = jnp.exp2((top[h] - high) * FACTOR)
-            p = jnp.exp2((s - high) * FACTOR)
+                scales.append(jnp.exp2((top[h] - high) * FACTOR))
+            ps = [jnp.exp2((s - high) * FACTOR) for s in scores[h]]
+            total = jnp.sum(functools.reduce(jnp.add, ps), axis=0, keepdims=True)
+            top[h] = high
+            tot[h] = total if own else tot[h] * scales[h] + total
+            weights.append(jnp.concatenate([p.astype(jnp.bfloat16) for p in ps], axis=0))
+        if ready is not None:
+            ready()
+        for h in range(kv_heads):
             mixed = jnp.dot(
-                p.astype(jnp.bfloat16), vb[j, :, h * HD:(h + 1) * HD],
-                preferred_element_type=jnp.float32)
-            top[h] = high
-            tot[h] = p if own else tot[h] * scale + p
-            acc[h] = mixed if own else acc[h] * scale + mixed
-
-    block(me, True)
+                jnp.concatenate([vb[j, h * HD:(h + 1) * HD, :] for j in js], axis=1),
+                weights[h], preferred_element_type=jnp.float32)
+            acc[h] = mixed if own else acc[h] * scales[h] + mixed
+
+    def keys_in(j):
+        arrived(kb, k_recv, j)
+
+    def values_in(j):
+        arrived(vb, v_recv, j)
+
+    def pass_on_block(ref, recv, j, relays):
+        block_copy(ref, recv, kv_fwd, j, partner).start()
+        if relays:
+            @pl.when(bearer)
+            def _():
+                block_copy(ref, recv, kv_fwd, j, me - 2).start()
+
+    def keys_on(j, relays=False):
+        keys_in(j)
+        pass_on_block(kb, k_recv, j, relays)
+
+    def values_on(j, relays=False):
+        values_in(j)
+        pass_on_block(vb, v_recv, j, relays)
+
+    @pl.when(core == 0)
+    def _():
+        attend([me], True)
 
     @pl.when(core == 1)
     def _():
-        arrived(kb, k_recv, me - 1)
-        arrived(vb, v_recv, me - 1)
-        block(me - 1, False)
+        keys_in(me - 1)
+        attend([me, me - 1], True, lambda: values_in(me - 1))
 
     count = jnp.minimum(chip, near)
 
@@ -219,51 +279,75 @@
     def other_of(i):
         return (chip - count + i) * 2 + 1 - core
 
-    def pass_keys(i, carry):
-        j = mine_of(i)
-        arrived(kb, k_recv, j)
-
-        block_copy(kb, k_recv, kv_fwd, j, partner).start()
+    def chip_step(i, carry):
+        mine, other = mine_of(i), other_of(i)
+        keys_on(mine)
+        attend([mine], False, lambda: values_on(mine))
+        keys_in(other)
+        attend([other], False, lambda: values_in(other))
         return carry
 
-    lax.fori_loop(0, count, pass_keys, 0)
-
-    def mine_step(i, carry):
-        j = mine_of(i)
-        arrived(vb, v_recv, j)
-        block_copy(vb, v_recv, kv_fwd, j, partner).start()
-        block(j, False)
-        return carry
-
-    lax.fori_loop(0, count, mine_step, 0)
-
-    def other_step(i, carry):
-        j = other_of(i)
-        arrived(kb, k_recv, j)
-        arrived(vb, v_recv, j)
-        block(j, False)
-        return carry
-
-    lax.fori_loop(0, count, other_step, 0)
-
-    @pl.when((core == 0) & (chip > near))
-    def _():
-        arrived(kb, k_recv, me - gap)
-        arrived(vb, v_recv, me - gap)
-        block(me - gap, False)
+    def far_step(js):
+        for j in js:
+            keys_in(j)
+
+        def ready():
+            for j in js:
+                values_in(j)
+
+        attend(js, False, ready)
+
+    if near == 2:
+        @pl.when(chip <= near)
+        def _():
+            lax.fori_loop(0, count, chip_step, 0)
+
+        @pl.when(chip > near)
+        def _():
+            mine, other = [mine_of(0), mine_of(1)], [other_of(0), other_of(1)]
+            for i, j in enumerate(mine):
+                keys_on(j, detour and i == 0)
+
+            def ready():
+                for i, j in enumerate(mine):
+                    values_on(j, detour and i == 0)
+
+            attend(mine, False, ready)
+
+            @pl.when(core == 0)
+            def _():
+                far_step(other + [me - gap])
+
+            @pl.when(core == 1)
+            def _():
+                far_step(other)
+    else:
+        lax.fori_loop(0, count, chip_step, 0)
+
+        @pl.when((core == 0) & (chip > near))
+        def _():
+            far_step([me - gap])
 
     for h in range(kv_heads):
-        result = (acc[h] / jnp.sum(tot[h], axis=1, keepdims=True)).astype(jnp.bfloat16)
+        result = acc[h] * (1.0 / tot[h])
         for g in range(group):
-            att[:, (h * group + g) * HD:(h * group + g + 1) * HD] = result[g * rows:(g + 1) * rows]
-
-    def piece_copy(p, way):
+            att[:, (h * group + g) * HD:(h * group + g + 1) * HD] = (
+                result[:, g * rows:(g + 1) * rows].T.astype(jnp.bfloat16))
+
+    def piece_copy(p, way, source=None, ctx=None):
         target = z + 1 if way == 0 else z - 1
         slot = p - SUB * target if way == 0 else SUB * (n_head - target) + p
         return pltpu.make_async_remote_copy(
-            src_ref=part.at[p], dst_ref=rbuf.at[way, p],
+            src_ref=part.at[p] if source is None else source, dst_ref=rbuf.at[way, p],
             send_sem=part_send.at[0], recv_sem=part_recv.at[slot],
-            device_id={"head": target}, device_id_type=MESH)
+            device_id={"head": target} if ctx is None else {"ctx": ctx, "head": target},
+            device_id_type=MESH)
+
+    def side_copy(p, i, ctx):
+        return pltpu.make_async_remote_copy(
+            src_ref=part.at[p], dst_ref=side.at[i],
+            send_sem=part_send.at[0], recv_sem=side_recv.at[i],
+            device_id={"ctx": ctx}, device_id_type=MESH)
 
     def piece_arrived(p, way):
         slot = p - SUB * z if way == 0 else SUB * (n_head - z) + p
@@ -277,20 +361,49 @@
         wo_copy(t).wait()
         for s in range(SUB):
             p = t * SUB + s
-            part[p] = jnp.dot(
-                att[...], wo[t, :, s * piece:(s + 1) * piece],
-                preferred_element_type=jnp.float32).astype(jnp.bfloat16)
+            if s % WIDE == 0:
+                product = jnp.dot(
+                    att[...], wo[t, :, s * piece:(s + WIDE) * piece],
+                    preferred_element_type=jnp.float32).astype(jnp.bfloat16)
+                for i in range(WIDE):
+                    part[p + i] = product[:, i * piece:(i + 1) * piece]
+
+            def send(way, t=t, p=p, s=s):
+                if not detour:
+                    piece_copy(p, way).start()
+                    return
+                nearest = t == (1 if way == 0 else n_head - 2)
+                given, held = nearest & giver & (s < SIDE), nearest & helper & (s >= SUB - SIDE)
+
+                @pl.when(jnp.logical_not(given | held))
+                def _():
+                    piece_copy(p, way).start()
+
+                if s < SIDE:
+                    @pl.when(given)
+                    def _():
+                        side_copy(p, s, me - n_ctx // 2).start()
 
             @pl.when((z == 0) & (t > 0))
-            def _():
-                piece_copy(p, 0).start()
+            def _(send=send):
+                send(0)
 
             @pl.when((z == n_head - 1) & (t < n_head - 1))
-            def _():
-                piece_copy(p, 1).start()
+            def _(send=send):
+                send(1)
         return carry
 
     lax.fori_loop(0, n_head, project, 0)
+
+    if detour:
+        for edge, way, t in ((0, 0, 1), (n_head - 1, 1, n_head - 2)):
+            @pl.when(helper & (z == edge))
+            def _(way=way, t=t):
+                for i in range(SIDE):
+                    side_copy(t * SUB + i, i, partner).wait_recv()
+                    piece_copy(t * SUB + i, way, side.at[i], me + n_ctx // 2).start()
+                for i in range(SUB - SIDE, SUB):
+                    piece_copy(t * SUB + i, way).start()
 
     def pass_on(p, way):
         piece_arrived(p, way)
@@ -298,8 +411,8 @@
         piece_copy(p, way).start()
 
     def relay(t, carry):
-        a = t - z
-        b = t - (n_head - 1 - z)
+        a = t - (SUB - 1) * z
+        b = t - (SUB - 1) * (n_head - 1 - z)
 
         @pl.when((z > 0) & (a >= 0) & (a < SUB * (n_head - 1 - z)))
         def _():
@@ -312,7 +425,7 @@
 
     @pl.when((z > 0) & (z < n_head - 1))
     def _():
-        lax.fori_loop(0, SUB * (n_head - 1) + n_head, relay, 0)
+        lax.fori_loop(0, (2 * SUB - 1) * (n_head - 1), relay, 0)
 
     def last(s, add_left, add_right):
         p = z * SUB + s
@@ -334,6 +447,10 @@
         return carry
 
     lax.fori_loop(0, count, drain_forward, 0)
+    if detour:
+        @pl.when(bearer)
+        def _():
+            drain_forward(0, 0)
 
     for which, left, right in ((z == 0, False, True), (z == n_head - 1, True, False),
                                ((z > 0) & (z < n_head - 1), True, True)):
@@ -352,6 +469,12 @@
         return carry
 
     lax.fori_loop(0, n_head * SUB, drain_piece, 0)
+
+    if detour:
+        @pl.when(helper & ((z == 0) | (z == n_head - 1)))
+        def _():
+            for i in range(SIDE):
+                side_copy(0, i, partner).wait_send()
 
 
 def solution(mesh):
@@ -382,23 +505,23 @@
                 pltpu.VMEM((n_head, q_width, SUB * piece), bf16),
                 pltpu.VMEM((1, rows), jnp.int32),
                 pltpu.VMEM((n_ctx, kv_heads * rows + TAIL, HD), bf16),
-                pltpu.VMEM((n_ctx, rows, kv_width), bf16),
+                pltpu.VMEM((n_ctx, kv_width, rows), bf16),
                 pltpu.VMEM((rows, q_width), f32),
                 pltpu.VMEM((rows, kv_width), f32),
                 pltpu.VMEM((rows, kv_width), f32),
-                pltpu.VMEM((heads, rows, HD), bf16),
+                pltpu.VMEM((kv_heads, group * rows, HD), bf16),
                 pltpu.VMEM((rows, HD), f32),
                 pltpu.VMEM((rows, HD), f32),
-                pltpu.VMEM((rows, rows), f32),
-                pltpu.VMEM((kv_heads, group * rows, rows), f32),
-                pltpu.VMEM((kv_heads, group * rows, rows), f32),
-                pltpu.VMEM((kv_heads, group * rows, HD), f32),
+                pltpu.VMEM((kv_heads, 1, group * rows), f32),
+                pltpu.VMEM((kv_heads, 1, group * rows), f32),
+                pltpu.VMEM((kv_heads, HD, group * rows), f32),
                 pltpu.VMEM((rows, q_width), bf16),
                 pltpu.VMEM((pieces, rows, piece), bf16),
                 pltpu.VMEM((2, pieces, rows, piece), bf16),
+                pltpu.VMEM((SIDE, rows, piece), bf16),
                 dma((STEPS,)), dma((STEPS,)), dma((STEPS // 2,)), dma((STEPS,)), dma((n_head,)), dma((1,)),
                 dma((1,)), dma((1,)), dma((reach,)), dma((reach,)),
-                dma((1,)), dma((SUB * (n_head + 1),)),
+                dma((1,)), dma((SUB * (n_head + 1),)), dma((SIDE,)),
             ],
             compiler_params=pltpu.CompilerParams(
                 collective_id=0, has_side_effects=True, vmem_limit_bytes=60 * 1024 * 1024),

time: 34.2 us -> 31.3 us (0.915); the launches traced: 33.7 us -> 31.2 us
  Pallas kernels: 33 us -> 30.5 us
    pallas_call x1, Pallas kernels: 33 us -> 30.5 us  [step(): pl.pallas_call(functools.partial(kernel, n_ctx, n_head, reach), out_shape...]
where the time goes in v2:
time: 31.3 us; the launch traced here: 31.2 us
  Pallas kernels  30.5 us (97%)
  local copies, waits for them, and re-layouts  0.71 us (2%)
    pallas_call x1, Pallas kernels, step(): pl.pallas_call(functools.partial(kernel, n_ctx, n_head, reach), out_shape...  30.5 us
    unnamed x1, local copies, waits for them, and re-layouts  0.71 us

profile of v2, /device:TPU:12, one launch (start us, length us, event | category | flops | bytes accessed | tf_op | source)
XLA Modules:
  0.0 31.2 jit_solution(2091896794546770970)
XLA Ops:
  0.0 30.5 %attention_layer.1 = bf16[128,1024]{1,0:T(8,128)(2,1)S(1)} custom-call(bf16[128,4096]{1,0:T(8,128)(2,1)} %tokens.1, bf16[4096,1024]{1,0:T(8,128)(2,1)} %w_query.1, bf16[4096,256]{1,0:T(8,128)(2,1)} %w_key.1, bf16[4096,256]{1,0:T(8,128)(2,1)} %w_value.1, bf16[1024,4096]{1,0:T(8,128)(2,1)} %w_out.1, s32[1,128]{1,0:T(1,128)} %bitcast.1), custom_call_target="tpu_custom_call" | custom-call | tf_op jit(solution)/shard_map/attention_layer/pallas_call | solution.py:495
  30.5 0.7 %copy.8 = bf16[128,1024]{1,0:T(8,128)(2,1)} copy(bf16[128,1024]{1,0:T(8,128)(2,1)S(1)} %attention_layer.1) | data formatting | bytes 524288

commit v3 on v2

--- a/solution.py
+++ b/solution.py
@@ -24,7 +24,7 @@
     tokens, w_query, w_key, w_value, w_out, docs, out,
     tok, wq, wk, wv, wo, doc, kb, vb, q_acc, k_acc, v_acc, q, cos_ref, sin_ref,
     top, tot, acc, att, part, rbuf, side,
-    tok_sem, wk_sem, wv_sem, wq_sem, wo_sem, doc_sem,
+    wq_sem, wo_sem, wv_sem, doc_sem,
     kv_send, kv_fwd, k_recv, v_recv, part_send, part_recv, side_recv,
 ):
     rows = tokens.shape[0]
@@ -44,7 +44,7 @@
 
     def tok_copy(c):
         return pltpu.make_async_copy(
-            tokens.at[:, c * step_rows:(c + 1) * step_rows], tok.at[c], tok_sem.at[c])
+            tokens.at[:, c * step_rows:(c + 1) * step_rows], tok.at[c], wq_sem.at[c])
 
     def rows_copy(src, dst, sem, c):
         size = dst.shape[1]
@@ -62,7 +62,7 @@
     doc_copy.start()
     for c in range(STEPS):
         tok_copy(c).start()
-        rows_copy(w_key, wk, wk_sem, c).start()
+        rows_copy(w_key, wk, wo_sem, c).start()
 
     barrier = pltpu.get_barrier_semaphore()
 
@@ -116,17 +116,18 @@
     sine = jnp.sin(angles)
     sin_ref[...] = jnp.where(index < HD // 2, -sine, sine)
 
+    rows_copy(w_value, wv, wv_sem, 0).start()
+
     def rotated(x):
         return (x * cos_ref[...] + pltpu.roll(x, HD // 2, 1) * sin_ref[...]).astype(jnp.bfloat16)
 
     for c in range(STEPS):
         tok_copy(c).wait()
-        rows_copy(w_key, wk, wk_sem, c).wait()
-        if c < STEPS // 2:
-            rows_copy(w_value, wv, wv_sem, c).start()
-        else:
-            for i in range(2 * c - STEPS, 2 * c - STEPS + 2):
-                rows_copy(w_query, wq, wq_sem, i).start()
+        rows_copy(w_key, wk, wo_sem, c).wait()
+        for i in ((), (0,), (1,), (2, 3))[c]:
+            rows_copy(w_query, wq, wq_sem, i).start()
+        if c == 0:
+            rows_copy(w_value, wv, wv_sem, 1).start()
         product = jnp.dot(tok[c], wk[c], preferred_element_type=jnp.float32)
         k_acc[...] = product if c == 0 else k_acc[...] + product
 
@@ -196,8 +197,8 @@
 
     for c in range(STEPS):
         rows_copy(w_query, wq, wq_sem, c).wait()
-        if c < n_head:
-            for k in range(c, n_head, STEPS):
+        if c == STEPS - 1:
+            for k in range(n_head):
                 wo_copy(owner_of(k)).start()
         product = jnp.dot(tok[c], wq[c], preferred_element_type=jnp.float32)
         q_acc[...] = product if c == 0 else q_acc[...] + product
@@ -372,17 +373,17 @@
                 if not detour:
                     piece_copy(p, way).start()
                     return
-                nearest = t == (1 if way == 0 else n_head - 2)
-                given, held = nearest & giver & (s < SIDE), nearest & helper & (s >= SUB - SIDE)
+                given = giver & (t == (2 if way == 0 else n_head - 3)) & (s >= SUB - SIDE)
+                held = helper & (t == (1 if way == 0 else n_head - 2))
 
                 @pl.when(jnp.logical_not(given | held))
                 def _():
                     piece_copy(p, way).start()
 
-                if s < SIDE:
+                if s >= SUB - SIDE:
                     @pl.when(given)
                     def _():
-                        side_copy(p, s, me - n_ctx // 2).start()
+                        side_copy(p, s - SUB + SIDE, me - n_ctx // 2).start()
 
             @pl.when((z == 0) & (t > 0))
             def _(send=send):
@@ -396,14 +397,15 @@
     lax.fori_loop(0, n_head, project, 0)
 
     if detour:
-        for edge, way, t in ((0, 0, 1), (n_head - 1, 1, n_head - 2)):
+        for edge, way, t, own in ((0, 0, 2, 1), (n_head - 1, 1, n_head - 3, n_head - 2)):
             @pl.when(helper & (z == edge))
-            def _(way=way, t=t):
+            def _(way=way, t=t, own=own):
                 for i in range(SIDE):
-                    side_copy(t * SUB + i, i, partner).wait_recv()
-                    piece_copy(t * SUB + i, way, side.at[i], me + n_ctx // 2).start()
-                for i in range(SUB - SIDE, SUB):
-                    piece_copy(t * SUB + i, way).start()
+                    p = t * SUB + SUB - SIDE + i
+                    side_copy(p, i, partner).wait_recv()
+                    piece_copy(p, way, side.at[i], me + n_ctx // 2).start()
+                for i in range(SUB):
+                    piece_copy(own * SUB + i, way).start()
 
     def pass_on(p, way):
         piece_arrived(p, way)
@@ -519,7 +521,7 @@
                 pltpu.VMEM((pieces, rows, piece), bf16),
                 pltpu.VMEM((2, pieces, rows, piece), bf16),
                 pltpu.VMEM((SIDE, rows, piece), bf16),
-                dma((STEPS,)), dma((STEPS,)), dma((STEPS // 2,)), dma((STEPS,)), dma((n_head,)), dma((1,)),
+                dma((STEPS,)), dma((max(STEPS, n_head),)), dma((STEPS // 2,)), dma((1,)),
                 dma((1,)), dma((1,)), dma((reach,)), dma((reach,)),
                 dma((1,)), dma((SUB * (n_head + 1),)), dma((SIDE,)),
             ],

time: 31.3 us -> 30.5 us (0.974)
  Pallas kernels: 30.5 us -> 29.7 us
    pallas_call x1, Pallas kernels: 30.5 us -> 29.7 us  [step(): pl.pallas_call(functools.partial(kernel, n_ctx, n_head, reach), out_shape...]
where the time goes in v3:
time: 30.5 us; the launch traced here: 30.4 us
  Pallas kernels  29.7 us (97%)
  local copies, waits for them, and re-layouts  0.71 us (2%)
    pallas_call x1, Pallas kernels, step(): pl.pallas_call(functools.partial(kernel, n_ctx, n_head, reach), out_shape...  29.7 us
    unnamed x1, local copies, waits for them, and re-layouts  0.71 us

profile of v3, /device:TPU:12, one launch (start us, length us, event | category | flops | bytes accessed | tf_op | source)
XLA Modules:
  0.0 30.4 jit_solution(12089037740225301875)
XLA Ops:
  0.0 29.7 %attention_layer.1 = bf16[128,1024]{1,0:T(8,128)(2,1)S(1)} custom-call(bf16[128,4096]{1,0:T(8,128)(2,1)} %tokens.1, bf16[4096,1024]{1,0:T(8,128)(2,1)} %w_query.1, bf16[4096,256]{1,0:T(8,128)(2,1)} %w_key.1, bf16[4096,256]{1,0:T(8,128)(2,1)} %w_value.1, bf16[1024,4096]{1,0:T(8,128)(2,1)} %w_out.1, s32[1,128]{1,0:T(1,128)} %bitcast.1), custom_call_target="tpu_custom_call" | custom-call | tf_op jit(solution)/shard_map/attention_layer/pallas_call | solution.py:497
  29.7 0.7 %copy.8 = bf16[128,1024]{1,0:T(8,128)(2,1)} copy(bf16[128,1024]{1,0:T(8,128)(2,1)S(1)} %attention_layer.1) | data formatting | bytes 524288

commit v4 on v3

--- a/solution.py
+++ b/solution.py
@@ -13,7 +13,7 @@
 STEPS = 4
 SUB = 4
 SIDE = 2
-WIDE = 2
+WIDTHS = (2, 0, 2, 0)
 TAIL = 16
 MESH = pl.DeviceIdType.MESH
 FACTOR = math.log2(math.e) / math.sqrt(HD)
@@ -66,19 +66,21 @@
 
     barrier = pltpu.get_barrier_semaphore()
 
+    last_near = jnp.minimum(chip + near, chips - 1)
+
     def greet(c, carry):
-        @pl.when(c != chip)
-        def _():
-            pl.semaphore_signal(
-                barrier, inc=1, device_id={"ctx": c * 2 + core}, device_id_type=MESH)
+        pl.semaphore_signal(
+            barrier, inc=1, device_id={"ctx": c * 2 + core}, device_id_type=MESH)
         return carry
 
-    lax.fori_loop(0, chips, greet, 0)
+    lax.fori_loop(jnp.maximum(chip - near, 0), chip, greet, 0)
     pl.semaphore_signal(barrier, inc=1, device_id={"ctx": partner}, device_id_type=MESH)
     gap = 2 * (near + 1) - 1
     detour = chips == 4 and n_head == 4
     helper, giver = chip == 0, chip == 2
-    greeted = chips + (z > 0).astype(jnp.int32) + (z < n_head - 1).astype(jnp.int32)
+    bearer = (chip == 3) & (core == 1)
+    greeted = (last_near - chip + 1 + (z > 0).astype(jnp.int32)
+               + (z < n_head - 1).astype(jnp.int32))
     if detour:
         for inner, edge in ((1, 0), (n_head - 2, n_head - 1)):
             @pl.when(giver & (z == inner))
@@ -87,7 +89,17 @@
                     barrier, inc=1, device_id={"ctx": me - n_ctx // 2, "head": edge},
                     device_id_type=MESH)
 
-        greeted = greeted + (helper & ((z == 0) | (z == n_head - 1))).astype(jnp.int32)
+        @pl.when(helper & ((z == 0) | (z == n_head - 1)))
+        def _():
+            greet(2, 0)
+
+        @pl.when((chip == 2) & (core == 1))
+        def _():
+            greet(3, 0)
+
+        greeted = greeted + (
+            (helper | giver) & ((z == 0) | (z == n_head - 1))).astype(jnp.int32) + (
+            bearer.astype(jnp.int32))
 
     @pl.when((core == 1) & (chip + near + 1 < chips))
     def _():
@@ -154,11 +166,7 @@
             send_sem=kv_send.at[0], recv_sem=recv.at[me - block - 1],
             device_id={"ctx": partner}, device_id_type=MESH).wait_recv()
 
-    last_near = jnp.minimum(chip + near, chips - 1)
-
     relayed = ((chip == 1) & (core == 1)).astype(jnp.int32)
-    bearer = (chip == 3) & (core == 1)
-
     def own_targets(act):
         def one(c, carry):
             act(c * 2 + core)
@@ -263,6 +271,11 @@
         values_in(j)
         pass_on_block(vb, v_recv, j, relays)
 
+    if detour:
+        @pl.when(bearer)
+        def _():
+            keys_on(me - 4, True)
+
     @pl.when(core == 0)
     def _():
         attend([me], True)
@@ -271,6 +284,11 @@
     def _():
         keys_in(me - 1)
         attend([me, me - 1], True, lambda: values_in(me - 1))
+
+    if detour:
+        @pl.when(bearer)
+        def _():
+            values_on(me - 4, True)
 
     count = jnp.minimum(chip, near)
 
@@ -299,19 +317,39 @@
         attend(js, False, ready)
 
     if near == 2:
-        @pl.when(chip <= near)
+        mine, other = [mine_of(0), mine_of(1)], [other_of(0), other_of(1)]
+
+        @pl.when(chip < near)
         def _():
             lax.fori_loop(0, count, chip_step, 0)
 
+        @pl.when(chip == near)
+        def _():
+            for j in mine:
+                keys_on(j)
+                attend([j], False, functools.partial(values_on, j))
+            far_step(other)
+
         @pl.when(chip > near)
         def _():
-            mine, other = [mine_of(0), mine_of(1)], [other_of(0), other_of(1)]
-            for i, j in enumerate(mine):
-                keys_on(j, detour and i == 0)
+            if not detour:
+                keys_on(mine[0])
+            else:
+                @pl.when(core == 0)
+                def _():
+                    keys_on(mine[0])
+
+            keys_on(mine[1])
 
             def ready():
-                for i, j in enumerate(mine):
-                    values_on(j, detour and i == 0)
+                if not detour:
+                    values_on(mine[0])
+                else:
+                    @pl.when(core == 0)
+                    def _():
+                        values_on(mine[0])
+
+                values_on(mine[1])
 
             attend(mine, False, ready)
 
@@ -362,11 +400,12 @@
         wo_copy(t).wait()
         for s in range(SUB):
             p = t * SUB + s
-            if s % WIDE == 0:
+            wide = WIDTHS[s]
+            if wide:
                 product = jnp.dot(
-                    att[...], wo[t, :, s * piece:(s + WIDE) * piece],
+                    att[...], wo[t, :, s * piece:(s + wide) * piece],
                     preferred_element_type=jnp.float32).astype(jnp.bfloat16)
-                for i in range(WIDE):
+                for i in range(wide):
                     part[p + i] = product[:, i * piece:(i + 1) * piece]
 
             def send(way, t=t, p=p, s=s):
@@ -416,13 +455,17 @@
         a = t - (SUB - 1) * z
         b = t - (SUB - 1) * (n_head - 1 - z)
 
-        @pl.when((z > 0) & (a >= 0) & (a < SUB * (n_head - 1 - z)))
-        def _():
+        def up():
             pass_on((n_head - 1 - a // SUB) * SUB + lax.rem(a, SUB), 0)
 
-        @pl.when((z < n_head - 1) & (b >= 0) & (b < SUB * z))
+        upward = (a >= 0) & (a < SUB * (n_head - 1 - z))
+        pl.when((z < n_head // 2) & upward)(up)
+
+        @pl.when((b >= 0) & (b < SUB * z))
         def _():
             pass_on(b, 1)
+
+        pl.when((z >= n_head // 2) & upward)(up)
         return carry
 
     @pl.when((z > 0) & (z < n_head - 1))

time: 30.5 us -> 30.5 us (level)
  no operation moved by 1% of the time
where the time goes in v4:
time: 30.5 us; the launch traced here: 30.1 us
  Pallas kernels  29.4 us (96%)
  local copies, waits for them, and re-layouts  0.71 us (2%)
    pallas_call x1, Pallas kernels, step(): pl.pallas_call(functools.partial(kernel, n_ctx, n_head, reach), out_shape...  29.4 us
    unnamed x1, local copies, waits for them, and re-layouts  0.71 us

profile of v4, /device:TPU:12, one launch (start us, length us, event | category | flops | bytes accessed | tf_op | source)
XLA Modules:
  0.0 30.1 jit_solution(4209886469504991575)
XLA Ops:
  0.0 29.4 %attention_layer.1 = bf16[128,1024]{1,0:T(8,128)(2,1)S(1)} custom-call(bf16[128,4096]{1,0:T(8,128)(2,1)} %tokens.1, bf16[4096,1024]{1,0:T(8,128)(2,1)} %w_query.1, bf16[4096,256]{1,0:T(8,128)(2,1)} %w_key.1, bf16[4096,256]{1,0:T(8,128)(2,1)} %w_value.1, bf16[1024,4096]{1,0:T(8,128)(2,1)} %w_out.1, s32[1,128]{1,0:T(1,128)} %bitcast.1), custom_call_target="tpu_custom_call" | custom-call | tf_op jit(solution)/shard_map/attention_layer/pallas_call | solution.py:540
  29.4 0.7 %copy.8 = bf16[128,1024]{1,0:T(8,128)(2,1)} copy(bf16[128,1024]{1,0:T(8,128)(2,1)S(1)} %attention_layer.1) | data formatting | bytes 524288
